TPU v7x, 32 devices: a whole 2x2x4 slice. The times are simulated.
32 devices in a mesh: row: 4 (over z), col: 8 (over y, x, core).
Axes of the slice: x: 2, y: 2, z: 4, core: 2. Of those that a mesh axis runs over, the one named last changes fastest.
Arguments:
- ainv_anc: bfloat16 [12288, 12288], P('row', 'col'), may hold values from -6 to 6
- l_panel: bfloat16 [1536, 12288], P('col', 'row'), may hold values from -0.109375 to 0.109375
- diag_inv: float32 [1536, 768], P('col', 'row'), may hold values from -6 to 6
- struct_mask: int32 [2, 96], replicated, may hold values 0 or 1
- pieces: float32 [1536, 32, 128], P(('row', 'col')), may hold values from -6 to 6
- tile_owner: int32 [1536, 1], P(('row', 'col')), may hold values from 0 to 31; in each aligned block of 48 rows (0 to 47, 48 to 95, ...) at most 3 rows name the same one
Outputs:
- ainv_upper: bfloat16 [1536, 12288], P('col', 'row')
- ainv_diag: float32 [1536, 768], P('col', 'row')
- moved: float32 [3072, 32, 128], P(('row', 'col'))
Inputs may be any that keep to these rules, and one draw needn't show every extreme that they name: `tile_owner`: among the 48 pieces of one device no owner is named more than 3 times, a bound that some block reaches.
All inputs are finite; a program needn't handle non-finite values.
Results may differ from a plain program's by a relative error of at most 0.015.
Values may be sent and summed in bfloat16 or wider, within the bound.
A program may use at most 128 MiB of HBM per device.

v0:
```python
import jax
import jax.numpy as jnp
from jax import lax
from jax.sharding import PartitionSpec as P

W = 768
AB = 128
SLOT = 3


def broadcast(value, axis, root):
    mine = lax.axis_index(axis) == root
    return lax.psum(jnp.where(mine, value, jnp.zeros_like(value)), axis)


def local(ainv_anc, l_panel, diag_inv, struct_mask, pieces, tile_owner):
    row_devices = lax.axis_size("row")
    col_devices = lax.axis_size("col")
    row_index = lax.axis_index("row")
    col_index = lax.axis_index("col")
    slab_rows = l_panel.shape[0]
    local_rows = l_panel.shape[1]
    cross_width = ainv_anc.shape[1]
    group_ratio = col_devices // row_devices
    supernode = col_index * slab_rows // W
    block_count = local_rows // AB
    keep_blocks = lax.dynamic_slice(
        struct_mask, (supernode, row_index * block_count), (1, block_count)
    )
    keep_rows = (
        jnp.broadcast_to(keep_blocks[:, :, None], (1, block_count, AB)).reshape(1, local_rows) > 0
    )
    masked = jnp.where(keep_rows, l_panel, jnp.zeros_like(l_panel))
    gathered = lax.all_gather(masked, "col", axis=0, tiled=True)
    offset = col_index % group_ratio * cross_width
    own_cross = lax.dynamic_slice_in_dim(gathered, offset, cross_width, 1)
    cross_rows = broadcast(own_cross, "row", col_index // group_ratio)
    product = lax.psum_scatter(
        lax.dot_general(
            cross_rows, ainv_anc, (((1,), (1,)), ((), ())), preferred_element_type=jnp.float32
        ).astype(jnp.bfloat16),
        "col",
        scatter_dimension=0,
        tiled=True,
    ).astype(jnp.float32)
    upper_rows = jnp.where(keep_rows, -product, jnp.zeros_like(product)).astype(jnp.bfloat16)
    own_block = lax.dynamic_slice_in_dim(gathered, supernode * W, W, 0)
    diag_part = lax.dot_general(
        upper_rows, own_block, (((1,), (1,)), ((), ())), preferred_element_type=jnp.float32
    )
    summed = lax.psum_scatter(
        diag_part.astype(jnp.bfloat16), "row", scatter_dimension=1, tiled=True
    ).astype(jnp.float32)
    ainv_diag = diag_inv - summed
    devices_all = row_devices * col_devices
    owners = tile_owner[:, 0]
    onehot = (owners[:, None] == jnp.arange(devices_all, dtype=jnp.int32)[None, :]).astype(
        jnp.int32
    )
    earlier = jnp.cumsum(onehot, axis=0) - onehot
    rank_in_dest = jnp.sum(earlier * onehot, axis=1)
    slot_index = owners * SLOT + rank_in_dest
    piece_rows = pieces.shape[1]
    piece_cols = pieces.shape[2]
    buffer = (
        jnp.zeros((devices_all * SLOT, piece_rows, piece_cols), jnp.float32)
        .at[slot_index]
        .set(pieces)
    )
    shaped = buffer.reshape(devices_all, SLOT, piece_rows, piece_cols)
    arrived = lax.all_to_all(
        shaped.astype(jnp.bfloat16), ("row", "col"), split_axis=0, concat_axis=0, tiled=True
    ).astype(shaped.dtype)
    moved_pieces = arrived.reshape(devices_all * SLOT, piece_rows, piece_cols)
    return (upper_rows, ainv_diag, moved_pieces)


def solution(mesh):
    in_specs = (
        P("row", "col"),
        P("col", "row"),
        P("col", "row"),
        P(),
        P(("row", "col"), None, None),
        P(("row", "col"), None),
    )
    out_specs = (P("col", "row"), P("col", "row"), P(("row", "col"), None, None))
    return jax.shard_map(local, mesh=mesh, in_specs=in_specs, out_specs=out_specs, check_vma=False)
```

profile of v0, /device:TPU:0, one launch (start us, length us, event | category | flops | bytes accessed | tf_op | source)
XLA Modules:
  0.0 382.2 jit_solution(5946898883278234848)
XLA Ops:
  7.2 0.8 compare_bitcast_fusion
  8.0 0.1 broadcast_bitcast_fusion
  8.1 2.4 broadcast_select_fusion
  10.5 0.0 all-reduce.2.cloned.1.call-start
  10.6 61.5 %all-gather.2.cloned.1.call-done = bf16[1536,3072]{1,0:T(8,128)(2,1)} async-done(((bf16[192,3072]{1,0:T(8,128)(2,1)}), bf16[1536,3072]{1,0:T(8,128)(2,1)}) %all-gather.2.cloned.1.call-update) | async-done | bytes 9437200 | tf_op jit(solution)/shard_map/all_gather | solution.py:34
  72.1 5.4 %dynamic-slice_select_fusion = bf16[1536,1536]{1,0:T(8,128)(2,1)} fusion(bf16[1536,3072]{1,0:T(8,128)(2,1)} %all-gather.2.cloned.1.call-done, s32[]{:T(128)S(6)} %select_n.53, pred[]{:T(512)S(6)} %eq.20), kind=kLoop, calls=%fused_computation.4 | loop fusion | flops 2359296 | bytes 9437189 | tf_op jit(solution)/shard_map/jit(_where)/select_n | solution.py:13
  77.5 172.1 %all-reduce.2.cloned.1.call-done = bf16[1536,1536]{1,0:T(8,128)(2,1)} async-done(((bf16[1536,1536]{1,0:T(8,128)(2,1)}), bf16[1536,1536]{1,0:T(8,128)(2,1)}) %all-reduce.2.cloned.1.call-update) | async-done | bytes 4718608 | tf_op jit(solution)/shard_map/psum | solution.py:13
  249.6 20.5 %convolution_convert_fusion = bf16[1536,3072]{1,0:T(8,128)(2,1)} fusion(bf16[1536,1536]{1,0:T(8,128)(2,1)} %all-reduce.2.cloned.1.call-done, bf16[3072,1536]{1,0:T(8,128)(2,1)} %param.6), kind=kOutput, calls=%fused_computation.1 | convolution fusion | flops 14500233216 | bytes 23592960 | tf_op jit(solution)/shard_map/dot_general | solution.py:39
  270.1 0.6 copy-done.3
  270.7 0.1 fusion.5
  270.8 0.1 reduce_window_sum.11
  270.9 0.2 select_reduce_fusion
  271.1 0.2 broadcast_in_dim.39
  271.3 2.0 scatter_fusion
  273.3 1.0 convert_element_type.31
  274.3 3.6 all-to-all-start
  277.9 68.1 %reduce-scatter.5.cloned.1.call-done = bf16[192,3072]{1,0:T(8,128)(2,1)} async-done(((bf16[1536,3072]{1,0:T(8,128)(2,1)}), bf16[192,3072]{1,0:T(8,128)(2,1)}) %reduce-scatter.5.cloned.1.call-update) | async-done | bytes 1179664 | tf_op jit(solution)/shard_map/reduce_scatter | solution.py:38
  346.0 1.6 select_convert_fusion
  347.6 4.5 %fusion.2 = bf16[192,768]{1,0:T(8,128)(2,1)S(1)} fusion(bf16[192,3072]{1,0:T(8,128)(2,1)S(1)} %select_convert_fusion, bf16[1536,3072]{1,0:T(8,128)(2,1)} %all-gather.2.cloned.1.call-done, s32[]{:T(128)S(6)} %select_n.56), kind=kOutput, calls=%fused_computation.6 | convolution fusion | flops 906117120 | bytes 6193156 | tf_op jit(solution)/shard_map/dot_general | solution.py:48
  352.1 0.9 copy.9
  353.1 1.4 bitcast_convert_fusion
  354.5 19.5 %reduce-scatter.7.cloned.1.call-done = bf16[192,192]{1,0:T(8,128)(2,1)} async-done(((bf16[768,192]{1,0:T(8,128)(2,1)}), bf16[192,192]{1,0:T(8,128)(2,1)}) %reduce-scatter.7.cloned.1.call-update) | async-done | bytes 73744
  374.0 1.0 copy.10
  375.0 0.7 convert_subtract_fusion
  (16 shorter events, 0.2 us)
Async XLA Ops:
  7.2 64.9 %all-gather.2.cloned.1.call-start = ((), (), s32[]{:S(2)}) async-start(), calls=%async_computation.3 | async-start | bytes 10616832 | tf_op jit(solution)/shard_map/all_gather | solution.py:34
  10.5 239.1 %all-reduce.2.cloned.1.call-start = ((), (), s32[]{:S(2)}) async-start(), calls=%async_computation.4 | async-start | bytes 9437184 | tf_op jit(solution)/shard_map/psum | solution.py:13
  77.5 268.6 %reduce-scatter.5.cloned.1.call-start = ((), (), s32[]{:S(2)}) async-start(), calls=%async_computation.5 | async-start | bytes 10616832 | tf_op jit(solution)/shard_map/reduce_scatter | solution.py:38
  270.1 0.7 copy-start.3
  270.1 1.2 copy-start.1
  274.3 78.7 %all-to-all-start = ((bf16[32,3,32,128]{3,2,1,0:T(8,128)(2,1)}), bf16[32,3,32,128]{3,2,1,0:T(8,128)(2,1)S(1)}, u32[]{:S(2)}, u32[]{:S(2)}) async-start(bf16[32,3,32,128]{3,2,1,0:T(8,128)(2,1)} %bitcast.5), calls=%async_computation.1 | async-start | bytes 1572864 | tf_op jit(solution)/shard_map/all_to_all | solution.py:71
  277.9 96.1 %reduce-scatter.7.cloned.1.call-start = ((), (), s32[]{:S(2)}) async-start(), calls=%async_computation.6 | async-start | bytes 491520
  347.6 4.5 %copy-start = (bf16[192,3072]{1,0:T(8,128)(2,1)}, bf16[192,3072]{1,0:T(8,128)(2,1)S(1)}, u32[]{:S(2)}) copy-start(bf16[192,3072]{1,0:T(8,128)(2,1)S(1)} %select_convert_fusion) | copy-start | bytes 3538948
  352.1 22.9 %copy-start.2 = (f32[192,192]{1,0:T(8,128)S(1)}, f32[192,192]{1,0:T(8,128)}, u32[]{:S(2)}) copy-start(f32[192,192]{1,0:T(8,128)} %param.8) | copy-start | bytes 442372
Sparse Core Ops, SparseCore 0:
  10.6 61.4 all-gather.1
  77.6 171.9 all-reduce.1
  270.2 75.7 reduce-scatter.4
  353.2 20.7 reduce-scatter.6
where the time goes:
time: 383 us; the launch traced here: 382 us
  waiting for transfers between devices  321 us (84%)
  matrix products  25 us (7%)
  between operations  13.9 us (4%)
  other arithmetic  13.6 us (4%)
  local copies, waits for them, and re-layouts  4.82 us (1%)
    psum x1, waiting for transfers between devices, broadcast(): return lax.psum(jnp.where(mine, value, jnp.zeros_like(value)), axis)  172 us
    reduce_scatter x1, waiting for transfers between devices, local(): lax.psum_scatter(lax.dot_general(cross_rows, ainv_anc, (((1,), (1,)), (()...  68.1 us
    all_gather x1, waiting for transfers between devices, local(): gathered = lax.all_gather(masked, 'col', axis=0, tiled=True)  61.5 us
    dot_general x1, matrix products, local(): lax.dot_general(cross_rows, ainv_anc, (((1,), (1,)), ((), ())), preferred...  20.5 us
    unnamed x5, waiting for transfers between devices  19.6 us
  transfers between devices with their start and end apart: 5, of which 4 were waited for; matrix products, arithmetic and copies ran while one was open for 3% of the time, Pallas kernels for 0%

commit v1 on v0

--- a/solution.py
+++ b/solution.py
@@ -10,7 +10,7 @@
 
 def broadcast(value, axis, root):
     mine = lax.axis_index(axis) == root
-    return lax.psum(jnp.where(mine, value, jnp.zeros_like(value)), axis)
+    return jnp.sum(lax.all_gather(jnp.where(mine, value, jnp.zeros_like(value)), axis), axis=0)
 
 
 def local(ainv_anc, l_panel, diag_inv, struct_mask, pieces, tile_owner):

time: 383 us -> 547 us (1.43)
  waiting for transfers between devices: 321 us -> 472 us
  other arithmetic: 13.6 us -> 27 us
    all_gather x0 -> x1, waiting for transfers between devices: none -> 323 us  [broadcast(): lax.all_gather(jnp.where(mine, value, jnp.zeros_like(value)), axis)]
    psum x1 -> x0, waiting for transfers between devices: 172 us -> none  [broadcast(): return lax.psum(jnp.where(mine, value, jnp.zeros_like(value)), axis)]
    reduce_sum x0 -> x1, other arithmetic: none -> 13.5 us  [broadcast(): jnp.sum(lax.all_gather(jnp.where(mine, value, jnp.zeros_like(value)), axi...]
  transfers between devices with their start and end apart: 5 -> 5, of which waited for: 4 -> 4; matrix products, arithmetic and copies ran while one was open for 3% -> 2% of each run, Pallas kernels for 0% -> 0%
where the time goes in v1:
time: 547 us; the launch traced here: 546 us
  waiting for transfers between devices  472 us (86%)
  other arithmetic  27 us (5%)
  matrix products  25 us (5%)
  between operations  13.9 us (3%)
    all_gather x1, waiting for transfers between devices, broadcast(): lax.all_gather(jnp.where(mine, value, jnp.zeros_like(value)), axis)  323 us
    reduce_scatter x1, waiting for transfers between devices, local(): lax.psum_scatter(lax.dot_general(cross_rows, ainv_anc, (((1,), (1,)), (()...  68.1 us
    all_gather x1, waiting for transfers between devices, local(): gathered = lax.all_gather(masked, 'col', axis=0, tiled=True)  61.5 us
    dot_general x1, matrix products, local(): lax.dot_general(cross_rows, ainv_anc, (((1,), (1,)), ((), ())), preferred...  20.5 us
    unnamed x5, waiting for transfers between devices  19.6 us
    reduce_sum x1, other arithmetic, broadcast(): jnp.sum(lax.all_gather(jnp.where(mine, value, jnp.zeros_like(value)), axi...  13.5 us
  transfers between devices with their start and end apart: 5, of which 4 were waited for; matrix products, arithmetic and copies ran while one was open for 2% of the time, Pallas kernels for 0%

profile of v1, /device:TPU:0, one launch (start us, length us, event | category | flops | bytes accessed | tf_op | source)
XLA Modules:
  0.0 546.1 jit_solution(10565487782699742555)
XLA Ops:
  7.2 0.8 compare_bitcast_fusion
  8.0 0.1 broadcast_bitcast_fusion
  8.1 2.4 broadcast_select_fusion
  10.6 61.5 %all-gather.4.cloned.1.call-done = bf16[1536,3072]{1,0:T(8,128)(2,1)} async-done(((bf16[192,3072]{1,0:T(8,128)(2,1)}), bf16[1536,3072]{1,0:T(8,128)(2,1)}) %all-gather.4.cloned.1.call-update) | async-done | bytes 9437200 | tf_op jit(solution)/shard_map/all_gather | solution.py:34
  72.1 5.3 dynamic-slice_select_fusion
  77.4 322.7 %all-gather.6.cloned.1.call-done = bf16[6144,1536]{1,0:T(8,128)(2,1)} async-done(((bf16[1536,1536]{1,0:T(8,128)(2,1)}), bf16[6144,1536]{1,0:T(8,128)(2,1)}) %all-gather.6.cloned.1.call-update) | async-done | bytes 18874384 | tf_op jit(solution)/shard_map/all_gather | solution.py:13
  400.1 13.5 %reduce_sum.23 = bf16[1536,1536]{1,0:T(8,128)(2,1)} reduce(bf16[4,1536,1536]{2,1,0:T(8,128)(2,1)} %bitcast.21, bf16[]{:T(256)} %constant.61.clone.1), dimensions={0}, to_apply=%region_0.1 | reduce | flops 7077888 | bytes 23592962 | tf_op jit(solution)/shard_map/reduce_sum | solution.py:13
  413.6 20.5 %convolution_convert_fusion = bf16[1536,3072]{1,0:T(8,128)(2,1)} fusion(bf16[1536,1536]{1,0:T(8,128)(2,1)} %reduce_sum.23, bf16[3072,1536]{1,0:T(8,128)(2,1)} %param.6), kind=kOutput, calls=%fused_computation.1 | convolution fusion | flops 14500233216 | bytes 23592960 | tf_op jit(solution)/shard_map/dot_general | solution.py:39
  434.2 0.6 copy-done.3
  434.8 0.1 fusion.5
  434.9 0.1 reduce_window_sum.11
  434.9 0.2 select_reduce_fusion
  435.1 0.2 broadcast_in_dim.39
  435.3 2.0 scatter_fusion
  437.4 1.0 convert_element_type.33
  438.4 3.4 all-to-all-start
  441.9 68.1 %reduce-scatter.5.cloned.1.call-done = bf16[192,3072]{1,0:T(8,128)(2,1)} async-done(((bf16[1536,3072]{1,0:T(8,128)(2,1)}), bf16[192,3072]{1,0:T(8,128)(2,1)}) %reduce-scatter.5.cloned.1.call-update) | async-done | bytes 1179664 | tf_op jit(solution)/shard_map/reduce_scatter | solution.py:38
  510.0 1.6 select_convert_fusion
  511.6 4.5 fusion.2
  516.1 0.9 copy.9
  517.0 1.4 bitcast_convert_fusion
  518.4 19.5 %reduce-scatter.7.cloned.1.call-done = bf16[192,192]{1,0:T(8,128)(2,1)} async-done(((bf16[768,192]{1,0:T(8,128)(2,1)}), bf16[192,192]{1,0:T(8,128)(2,1)}) %reduce-scatter.7.cloned.1.call-update) | async-done | bytes 73744
  537.9 1.0 copy.10
  538.9 0.7 convert_subtract_fusion
  (17 shorter events, 0.3 us)
Async XLA Ops:
  7.2 64.9 %all-gather.4.cloned.1.call-start = ((), (), s32[]{:S(2)}) async-start(), calls=%async_computation.3 | async-start | bytes 10616832 | tf_op jit(solution)/shard_map/all_gather | solution.py:34
  10.5 389.6 %all-gather.6.cloned.1.call-start = ((), (), s32[]{:S(2)}) async-start(), calls=%async_computation.5 | async-start | bytes 23592960 | tf_op jit(solution)/shard_map/all_gather | solution.py:13
  77.4 432.6 %reduce-scatter.5.cloned.1.call-start = ((), (), s32[]{:S(2)}) async-start(), calls=%async_computation.4 | async-start | bytes 10616832 | tf_op jit(solution)/shard_map/reduce_scatter | solution.py:38
  434.1 0.7 copy-start.3
  434.1 1.2 copy-start.1
  438.4 78.6 %all-to-all-start = ((bf16[32,3,32,128]{3,2,1,0:T(8,128)(2,1)}), bf16[32,3,32,128]{3,2,1,0:T(8,128)(2,1)S(1)}, u32[]{:S(2)}, u32[]{:S(2)}) async-start(bf16[32,3,32,128]{3,2,1,0:T(8,128)(2,1)} %bitcast.6), calls=%async_computation.1 | async-start | bytes 1572864 | tf_op jit(solution)/shard_map/all_to_all | solution.py:71
  441.8 96.1 %reduce-scatter.7.cloned.1.call-start = ((), (), s32[]{:S(2)}) async-start(), calls=%async_computation.6 | async-start | bytes 491520
  511.5 4.5 copy-start
  516.0 22.9 %copy-start.2 = (f32[192,192]{1,0:T(8,128)S(1)}, f32[192,192]{1,0:T(8,128)}, u32[]{:S(2)}) copy-start(f32[192,192]{1,0:T(8,128)} %param.8) | copy-start | bytes 442372
Sparse Core Ops, SparseCore 0:
  10.6 61.4 all-gather.3
  77.5 322.5 all-gather.5
  434.3 75.6 reduce-scatter.4
  517.1 20.7 reduce-scatter.6
